TPU v7x, 256 devices: a whole 4x4x8 slice. The times are simulated.
256 devices in a mesh: emb: 16 (over z, core), dp: 16 (over x, y).
Axes of the slice: x: 4, y: 4, z: 8, core: 2. Of those that a mesh axis runs over, the one named last changes fastest.
Arguments:
- embeddings: bfloat16 [512, 1024, 256], P('emb', 'dp'), may hold values from -9 to 9
- machine_projection: bfloat16 [512, 32], replicated, may hold values from -0.015625 to 0.015625
- w_lcb: bfloat16 [512, 512], P('dp'), may hold values from -0.25 to 0.25
- w_fmb: bfloat16 [32, 256], replicated, may hold values from -1 to 1
- ln_gain: float32 [512, 256], P('emb'), may hold values from 0.5 to 1.5
- ln_bias: float32 [512, 256], P('emb'), may hold values from -1.8 to 1.8
Outputs:
- layer_out: bfloat16 [512, 1024, 256], P('emb', 'dp')
All inputs are finite; a program needn't handle non-finite values.
Results may differ from a plain program's by a relative error of at most 0.007.
Values may be sent and summed in bfloat16 or wider, within the bound.
A program may use at most 64 MiB of HBM per device.

v0:
```python
import jax
import jax.numpy as jnp
from jax import lax
from jax.sharding import Mesh
from jax.sharding import PartitionSpec as P

DP = ("dp_0", "dp_1")


def gathered_by_axis(shard, axes, dim):
    if not axes:
        return shard
    nearer = lax.all_gather(shard, axes[-1], axis=dim, tiled=True)
    return gathered_by_axis(nearer, axes[:-1], dim)


def in_one_piece(arrays, axis, dim, along):
    both = jnp.concatenate(arrays, axis=along)
    result, at, gathered = (lax.all_gather(both, axis, axis=dim, tiled=True), 0, [])
    for a in arrays:
        gathered.append(lax.slice_in_dim(result, at, at + a.shape[along], axis=along))
        at += a.shape[along]
    return tuple(gathered)


def finish_block(embeddings, compressed, summed_values, w_fmb):
    row_count, samples, width = embeddings.shape
    factor_dimension = summed_values.shape[1]
    factor_matrix = summed_values.astype(jnp.bfloat16)
    inner_product = jnp.einsum(
        "gue,ufe->guf", embeddings, factor_matrix, preferred_element_type=jnp.float32
    ).astype(jnp.bfloat16)
    fmb_out = jnp.dot(
        inner_product.reshape(row_count * samples, factor_dimension),
        w_fmb,
        preferred_element_type=jnp.float32,
    ).reshape(row_count, samples, width)
    return embeddings.astype(jnp.float32) + compressed + fmb_out


def body(embeddings, machine_projection, w_lcb, w_fmb, ln_gain, ln_bias):
    local_rows, samples, width = embeddings.shape
    weights_full = gathered_by_axis(w_lcb, DP, 0)
    emb_count = weights_full.shape[0]
    entries = jnp.float32(emb_count * width)
    regrouped = lax.all_to_all(embeddings, "emb", split_axis=1, concat_axis=0, tiled=True)
    gain_full, bias_full = in_one_piece((ln_gain, ln_bias), "emb", 0, 1)
    share = regrouped.shape[1]
    compressed = jnp.dot(
        weights_full,
        regrouped.reshape(emb_count, share * width),
        preferred_element_type=jnp.float32,
    ).reshape(emb_count, share, width)
    summed_values = jnp.einsum(
        "slc,sf->lfc", regrouped, machine_projection, preferred_element_type=jnp.float32
    )
    mixed = finish_block(regrouped, compressed, summed_values, w_fmb)
    average = jnp.sum(mixed, axis=(0, 2)) / entries
    centered = mixed - average[None, :, None]
    spread = jnp.sum(centered * centered, axis=(0, 2)) / entries
    scaled = centered * lax.rsqrt(spread + 1e-05)[None, :, None]
    result = (scaled * gain_full[:, None, :] + bias_full[:, None, :]).astype(jnp.bfloat16)
    return lax.all_to_all(result, "emb", split_axis=0, concat_axis=1, tiled=True)


def solution(mesh):
    finer = Mesh(mesh.devices.reshape(mesh.shape["emb"], 4, 4), ("emb", "dp_0", "dp_1"))
    placed = (P("emb", DP, None), P(), P(DP, None), P(), P("emb", None), P("emb", None))
    return jax.shard_map(
        body, mesh=finer, in_specs=placed, out_specs=P("emb", DP, None), check_vma=False
    )
```

profile of v0, /device:TPU:1, one launch (start us, length us, event | category | flops | bytes accessed | tf_op | source)
XLA Modules:
  0.0 107.5 jit_solution(1322454663124096439)
XLA Ops:
  6.5 0.0 copy-start
  6.5 0.0 copy-start.3
  6.5 0.0 copy-start.2
  6.5 0.0 copy-start.1
  6.5 2.8 %copy.14 = bf16[32,64,256]{2,0,1:T(8,128)(2,1)} copy(bf16[32,64,256]{2,1,0:T(8,128)(2,1)} %param.6) | data formatting | bytes 2097152 | tf_op args[0]
  9.3 10.0 %all-to-all-start = ((bf16[32,64,256]{2,0,1:T(8,128)(2,1)}), bf16[32,64,256]{2,0,1:T(8,128)(2,1)S(1)}, u32[]{:S(2)}, u32[]{:S(2)}) async-start(bf16[32,64,256]{2,0,1:T(8,128)(2,1)} %copy.14), calls=%async_computation | async-start | bytes 2097152 | tf_op jit(solution)/shard_map/all_to_all | solution.py:46
  19.3 0.0 all-gather.2.cloned.1.call-start
  19.3 0.0 copy-done.3
  19.4 0.0 copy-done.2
  19.4 0.6 pad_maximum_fusion
  20.0 0.0 all-gather.2.cloned.1.call-update
  20.0 0.0 copy-done.1
  20.0 10.5 %all_gather.9 = bf16[128,512]{1,0:T(8,128)(2,1)S(1)} all-gather(bf16[32,512]{1,0:T(8,128)(2,1)S(1)} %copy-done.1), channel_id=1, replica_groups=mesh['emb'=16,'dp_0'=4,'dp_1'=4] {'dp_1'}, dimensions={0}, use_global_device_ids=true | all-gather | bytes 163840 | tf_op jit(solution)/shard_map/all_gather | solution.py:13
  30.6 11.8 %all_gather.10 = bf16[512,512]{1,0:T(8,128)(2,1)} all-gather(bf16[128,512]{1,0:T(8,128)(2,1)S(1)} %all_gather.9), channel_id=1, replica_groups=mesh['emb'=16,'dp_0'=4,'dp_1'=4] {'dp_0'}, dimensions={0}, use_global_device_ids=true | all-gather | bytes 655360 | tf_op jit(solution)/shard_map/all_gather | solution.py:13
  42.4 6.6 %all-to-all-done = bf16[32,64,256]{2,0,1:T(8,128)(2,1)S(1)} async-done(((bf16[32,64,256]{2,0,1:T(8,128)(2,1)}), bf16[32,64,256]{2,0,1:T(8,128)(2,1)S(1)}, u32[]{:S(2)}, u32[]{:S(2)}) %all-to-all-start) | async-done | bytes 1048608 | tf_op jit(solution)/shard_map/all_to_all | solution.py:46
  48.9 0.9 copy.23
  49.8 0.2 copy.16
  50.0 0.2 copy.20
  50.2 0.5 copy.17
  50.8 0.0 copy-done
  50.8 0.3 fusion.1
  51.1 0.0 copy-start.4
  51.1 3.2 %fusion.2 = f32[512,4,256]{2,0,1:T(8,128)} fusion(bf16[4,256,512]{2,1,0:T(8,128)(2,1)S(1)} %bitcast.41, bf16[512,512]{1,0:T(8,128)(2,1)} %all_gather.10), kind=kOutput, calls=%fused_computation.7 | convolution fusion | flops 536870912 | bytes 3670016 | tf_op jit(solution)/shard_map/dot_general | solution.py:49
  54.2 0.0 copy-done.4
  54.2 2.5 %fusion.7 = (f32[4]{0:T(128)S(1)}, f32[512,4,256]{2,0,1:T(8,128)S(1)}) fusion(bf16[32,256]{1,0:T(8,128)(2,1)S(1)} %copy-done.4, bf16[4,32,256]{2,1,0:T(8,128)(2,1)S(1)} %fusion.1, bf16[512,4,256]{2,0,1:T(8,128)(2,1)S(1)} %bitcast.40, f32[512,4,256]{2,0,1:T(8,128)} %fusion.2), kind=kOutput, calls=%fused_computation.16 | convolution fusion | flops 69271552 | bytes 5324816 | tf_op jit(solution)/shard_map/dot_general | solution.py:33
  56.8 0.4 multiply_reduce_fusion
  57.2 6.8 %all-gather.2.cloned.1.call-done = f32[512,512]{1,0:T(8,128)} async-done(((f32[32,512]{1,0:T(8,128)}), f32[512,512]{1,0:T(8,128)}) %all-gather.2.cloned.1.call-update) | async-done | bytes 1048592 | tf_op jit(solution)/shard_map/all_gather | solution.py:19
  64.0 1.3 %fusion.6 = (f32[512,256]{1,0:T(8,128)S(1)}, f32[512,256]{1,0:T(8,128)S(1)}) fusion(f32[512,512]{1,0:T(8,128)} %all-gather.2.cloned.1.call-done), kind=kLoop, calls=%fused_computation.15 | loop fusion | bytes 2097152 | tf_op jit(solution)/shard_map/slice | solution.py:21
  65.3 0.5 add_convert_fusion
  65.8 0.8 copy.18
  66.6 32.3 %all_to_all.36 = bf16[512,4,256]{2,1,0:T(4,128)(2,1)S(1)} all-to-all(bf16[512,4,256]{2,1,0:T(4,128)(2,1)S(1)} %copy.18), channel_id=1, replica_groups=mesh['emb'=16,'dp_0'=4,'dp_1'=4] {'emb'}, dimensions={0} | all-to-all | bytes 2097152 | tf_op jit(solution)/shard_map/all_to_all | solution.py:63
  98.9 0.5 copy.19
  99.5 1.1 %all_to_all.33 = bf16[32,64,256]{2,1,0:T(8,128)(2,1)} reshape(bf16[32,16,4,256]{3,2,1,0:T(4,128)(2,1)S(1)} %copy.19) | data formatting | bytes 2097152 | tf_op jit(solution)/shard_map/all_to_all | solution.py:63
  (2 shorter events, 0.0 us)
Async XLA Ops:
  6.5 44.2 %copy-start = (bf16[512,32]{0,1:T(8,128)(2,1)S(1)}, bf16[512,32]{0,1:T(8,128)(2,1)}, u32[]{:S(2)}) copy-start(bf16[512,32]{0,1:T(8,128)(2,1)} %param.7) | copy-start | bytes 98308
  6.5 12.8 %copy-start.3 = (f32[32,256]{1,0:T(8,128)S(1)}, f32[32,256]{1,0:T(8,128)}, u32[]{:S(2)}) copy-start(f32[32,256]{1,0:T(8,128)} %param.10) | copy-start | bytes 98308
  6.5 12.8 %copy-start.2 = (f32[32,256]{1,0:T(8,128)S(1)}, f32[32,256]{1,0:T(8,128)}, u32[]{:S(2)}) copy-start(f32[32,256]{1,0:T(8,128)} %param.11) | copy-start | bytes 98308
  6.5 13.5 %copy-start.1 = (bf16[32,512]{1,0:T(8,128)(2,1)S(1)}, bf16[32,512]{1,0:T(8,128)(2,1)}, u32[]{:S(2)}) copy-start(bf16[32,512]{1,0:T(8,128)(2,1)} %param.8) | copy-start | bytes 98308
  9.3 39.6 %all-to-all-start = ((bf16[32,64,256]{2,0,1:T(8,128)(2,1)}), bf16[32,64,256]{2,0,1:T(8,128)(2,1)S(1)}, u32[]{:S(2)}, u32[]{:S(2)}) async-start(bf16[32,64,256]{2,0,1:T(8,128)(2,1)} %copy.14), calls=%async_computation | async-start | bytes 2097152 | tf_op jit(solution)/shard_map/all_to_all | solution.py:46
  19.3 44.7 %all-gather.2.cloned.1.call-start = ((), (), s32[]{:S(2)}) async-start(), calls=%async_computation.2 | async-start | bytes 1114112 | tf_op jit(solution)/shard_map/all_gather | solution.py:19
  51.1 3.2 %copy-start.4 = (bf16[32,256]{1,0:T(8,128)(2,1)S(1)}, bf16[32,256]{1,0:T(8,128)(2,1)}, u32[]{:S(2)}) copy-start(bf16[32,256]{1,0:T(8,128)(2,1)} %param.9) | copy-start | bytes 49156
Sparse Core Ops, SparseCore 0:
  21.9 42.0 all-gather.1
where the time goes:
time: 108 us; the launch traced here: 107 us
  blocking collectives  54.6 us (51%)
  between operations  13.5 us (12%)
  waiting for transfers between devices  13.4 us (12%)
  starting transfers between devices  10 us (9%)
  local copies, waits for them, and re-layouts  8.38 us (8%)
  matrix products  5.97 us (6%)
  other arithmetic  1.6 us (1%)
    all_to_all x1, blocking collectives, body(): lax.all_to_all(result, 'emb', split_axis=0, concat_axis=1, tiled=True)  32.3 us
    all_gather x2, blocking collectives, gathered_by_axis(): nearer = lax.all_gather(shard, axes[-1], axis=dim, tiled=True)  22.3 us
    all_to_all x1, starting transfers between devices, body(): lax.all_to_all(embeddings, 'emb', split_axis=1, concat_axis=0, tiled=True)  9.97 us
    all_gather x1, waiting for transfers between devices, in_one_piece(): lax.all_gather(both, axis, axis=dim, tiled=True)  6.8 us
    all_to_all x1, waiting for transfers between devices, body(): lax.all_to_all(embeddings, 'emb', split_axis=1, concat_axis=0, tiled=True)  6.56 us
    dot_general x1, matrix products, body(): jnp.dot(weights_full, regrouped.reshape(emb_count, share * width), prefer...  3.15 us
    unnamed x12, local copies, waits for them, and re-layouts  3.03 us
    dot_general x1, matrix products, finish_block(): jnp.dot(inner_product.reshape(row_count * samples, factor_dimension), w_f...  2.54 us
  transfers between devices with their start and end apart: 2, of which 2 were waited for; matrix products, arithmetic and copies ran while one was open for 8% of the time, Pallas kernels for 0%

commit v1 on v0

v1 whole, which is shorter than its diff:
```python
import functools

import jax
import jax.numpy as jnp
from jax import lax
from jax.experimental import pallas as pl
from jax.experimental.pallas import tpu as pltpu
from jax.sharding import PartitionSpec as P

MESH = pl.DeviceIdType.MESH
PEERS = ((0, 1),) + tuple((d, c) for d in (1, 7, 2, 6, 3, 5, 4) for c in (0, 1))
PITCH = 24


def kernel(
    emb_ref, mp_ref, w_ref, wf_ref, g_ref, b_ref, out_ref,
    ebuf, stage, sendbuf, xbuf, wfull, rbuf, ybuf, mixed, wf_v, g_v, b_v,
    load_sem, small_sem, in_send, in_recv, out_send, out_recv, w_send, w_recv,
):
    e = lax.axis_index("emb")
    dp = lax.axis_index("dp")
    z, c = e // 2, e % 2
    rows, samples, width = ebuf.shape
    chunks, group = sendbuf.shape[0], sendbuf.shape[1]
    emb_count = xbuf.shape[1]
    n_dp = w_send.shape[0] + 1

    def peer(d, cc):
        return lax.rem(z + d, 8) * 2 + lax.rem(c + cc, 2)

    barrier = pltpu.get_barrier_semaphore()
    for d, cc in PEERS:
        pl.semaphore_signal(barrier, inc=1, device_id={"emb": peer(d, cc)}, device_id_type=MESH)
    for k in range(1, n_dp):
        pl.semaphore_signal(barrier, inc=1, device_id={"dp": lax.rem(dp + k, n_dp)}, device_id_type=MESH)

    def load(s):
        part = pl.ds(s * group, group)
        return pltpu.make_async_copy(emb_ref.at[:, part], ebuf.at[:, part], load_sem.at[s])

    my_w = pl.ds(pl.multiple_of(dp * rows, rows), rows)
    load(0).start()
    own_w = pltpu.make_async_copy(w_ref, wfull.at[my_w], small_sem.at[0])
    own_w.start()
    for s in range(1, chunks):
        load(s).start()
    small = [
        pltpu.make_async_copy(a, v, small_sem.at[1 + i])
        for i, (a, v) in enumerate(((mp_ref, wfull.at[pl.ds(emb_count, mp_ref.shape[0])]), (wf_ref, wf_v), (g_ref, g_v), (b_ref, b_v)))
    ]
    for copy in small:
        copy.start()

    my_rows = pl.ds(pl.multiple_of(e * rows, rows), rows)

    def prepare(s):
        load(s).wait()
        for n in range(rows):
            block = ebuf[n, pl.ds(pl.multiple_of(s * group, group), group), :].astype(jnp.float32)
            for h in range(2):
                stage[h, pl.ds(n * PITCH, group), :] = block[:, h * 128 : (h + 1) * 128]
        for b in range(group):
            for h in range(2):
                sendbuf[s, b, :, pl.ds(h * 128, 128)] = stage[h, pl.ds(b, rows, stride=PITCH), :].astype(jnp.bfloat16)
        xbuf[s, my_rows, :] = sendbuf[s, e]

    def send_in(s):
        for i, (d, cc) in enumerate(PEERS):
            j = peer(d, cc)
            pltpu.make_async_remote_copy(
                src_ref=sendbuf.at[s, j], dst_ref=xbuf.at[s, my_rows],
                send_sem=in_send.at[s], recv_sem=in_recv.at[s],
                device_id={"emb": j}, device_id_type=MESH,
            ).start()

    def w_copy(k):
        return pltpu.make_async_remote_copy(
            src_ref=wfull.at[my_w], dst_ref=wfull.at[my_w], send_sem=w_send.at[k - 1], recv_sem=w_recv,
            device_id={"dp": lax.rem(dp + k, n_dp)}, device_id_type=MESH,
        )

    prepare(0)
    own_w.wait()
    pl.semaphore_wait(barrier, len(PEERS) + n_dp - 1)
    send_in(0)
    for k in range(1, n_dp):
        w_copy(k).start()

    def feed(s, carry):
        prepare(s)
        send_in(s)
        return carry

    lax.fori_loop(1, chunks, feed, 0)

    for copy in small:
        copy.wait()
    others = pl.ds(0, emb_count - rows)
    pltpu.make_async_copy(wfull.at[others], wfull.at[others], w_recv).wait()

    block = 128
    entries = jnp.float32(emb_count * width)

    def mix(s, carry):
        pltpu.make_async_copy(xbuf.at[s, others], xbuf.at[s, others], in_recv.at[s]).wait()
        x = xbuf[s]
        factor = jnp.dot(wfull[pl.ds(emb_count, 32), :], x, preferred_element_type=jnp.float32).astype(jnp.bfloat16)
        total = jnp.zeros((8, width), jnp.float32)
        for i in range(emb_count // block):
            part = pl.ds(i * block, block)
            xb = xbuf[s, part, :]
            inner = lax.dot_general(xb, factor, (((1,), (1,)), ((), ())), preferred_element_type=jnp.float32).astype(jnp.bfloat16)
            m = jnp.dot(wfull[part, :], x, preferred_element_type=jnp.float32)
            m = m + xb.astype(jnp.float32) + jnp.dot(inner, wf_v[...], preferred_element_type=jnp.float32)
            mixed[part, :] = m
            total = total + jnp.sum(m.reshape(block // 8, 8, width), axis=0)
        average = jnp.sum(total, keepdims=True) / entries
        square = jnp.zeros((8, width), jnp.float32)
        for i in range(emb_count // block):
            centered = mixed[pl.ds(i * block, block), :] - average
            square = square + jnp.sum((centered * centered).reshape(block // 8, 8, width), axis=0)
        scale = lax.rsqrt(jnp.sum(square, keepdims=True) / entries + 1e-05)
        for i in range(emb_count // block):
            part = pl.ds(i * block, block)
            rbuf[s, part, :] = ((mixed[part, :] - average) * scale).astype(jnp.bfloat16)
        ybuf[s, e] = rbuf[s, my_rows, :]
        for i, (d, cc) in enumerate(PEERS):
            j = peer(d, cc)
            pltpu.make_async_remote_copy(
                src_ref=rbuf.at[s, pl.ds(pl.multiple_of(j * rows, rows), rows)], dst_ref=ybuf.at[s, e],
                send_sem=out_send.at[s], recv_sem=out_recv.at[s],
                device_id={"emb": j}, device_id_type=MESH,
            ).start()
        return carry

    lax.fori_loop(0, chunks, mix, 0)

    fifteen = pl.ds(0, group - 1)

    def finish(s, carry):
        pltpu.make_async_copy(ybuf.at[s, fifteen], ybuf.at[s, fifteen], out_recv.at[s]).wait()
        part = pl.ds(pl.multiple_of(s * group, group), group)
        for b in range(group):
            y = ybuf[s, b].astype(jnp.float32) * g_v[...] + b_v[...]
            for h in range(2):
                stage[h, pl.ds(b, rows, stride=PITCH), :] = y[:, h * 128 : (h + 1) * 128]
        for n in range(rows):
            for h in range(2):
                out_ref[n, part, pl.ds(h * 128, 128)] = stage[h, pl.ds(n * PITCH, group), :].astype(jnp.bfloat16)
        return carry

    lax.fori_loop(0, chunks, finish, 0)

    def drain(s, carry):
        pltpu.make_async_copy(sendbuf.at[s, fifteen], sendbuf.at[s, fifteen], in_send.at[s]).wait()
        pltpu.make_async_copy(ybuf.at[s, fifteen], ybuf.at[s, fifteen], out_send.at[s]).wait()
        return carry

    lax.fori_loop(0, chunks, drain, 0)
    for k in range(1, n_dp):
        w_copy(k).wait_send()


def body(embeddings, machine_projection, w_lcb, w_fmb, ln_gain, ln_bias):
    rows, samples, width = embeddings.shape
    emb_count, rank = machine_projection.shape
    group = emb_count // rows
    chunks = samples // group
    hbm = pl.BlockSpec(memory_space=pltpu.HBM)
    bf16, f32 = jnp.bfloat16, jnp.float32
    return pl.pallas_call(
        kernel,
        out_shape=jax.ShapeDtypeStruct((rows, samples, width), bf16),
        in_specs=[hbm] * 6,
        out_specs=pl.BlockSpec(memory_space=pltpu.VMEM),
        scratch_shapes=[
            pltpu.VMEM((rows, samples, width), bf16),
            pltpu.VMEM((2, rows * PITCH, 128), f32),
            pltpu.VMEM((chunks, group, rows, width), bf16),
            pltpu.VMEM((chunks, emb_count, width), bf16),
            pltpu.VMEM((emb_count + rank, emb_count), bf16),
            pltpu.VMEM((chunks, emb_count, width), bf16),
            pltpu.VMEM((chunks, group, rows, width), bf16),
            pltpu.VMEM((emb_count, width), f32),
            pltpu.VMEM(w_fmb.shape, bf16),
            pltpu.VMEM(ln_gain.shape, f32),
            pltpu.VMEM(ln_bias.shape, f32),
            pltpu.SemaphoreType.DMA((chunks,)),
            pltpu.SemaphoreType.DMA((5,)),
            pltpu.SemaphoreType.DMA((chunks,)),
            pltpu.SemaphoreType.DMA((chunks,)),
            pltpu.SemaphoreType.DMA((chunks,)),
            pltpu.SemaphoreType.DMA((chunks,)),
            pltpu.SemaphoreType.DMA((emb_count // w_lcb.shape[0] - 1,)),
            pltpu.SemaphoreType.DMA,
        ],
        compiler_params=pltpu.CompilerParams(
            collective_id=0, has_side_effects=True, vmem_limit_bytes=67043328
        ),
        name="wukong",
    )(embeddings, machine_projection.T, w_lcb, w_fmb, ln_gain, ln_bias)


def solution(mesh):
    placed = (P("emb", "dp", None), P(), P("dp", None), P(), P("emb", None), P("emb", None))
    return jax.shard_map(
        body, mesh=mesh, in_specs=placed, out_specs=P("emb", "dp", None), check_vma=False
    )
```

time: 108 us -> 63.2 us (0.59)
  Pallas kernels: 0 us -> 60.8 us
  blocking collectives: 54.6 us -> 0 us
  between operations: 13.5 us -> 0.01 us
  waiting for transfers between devices: 13.4 us -> 0 us
  starting transfers between devices: 10 us -> 0 us
  local copies, waits for them, and re-layouts: 8.38 us -> 2.3 us
  matrix products: 5.97 us -> 0 us
  other arithmetic: 1.6 us -> 0 us
    pallas_call x0 -> x1, Pallas kernels: none -> 60.8 us  [body(): pl.pallas_call(kernel, out_shape=jax.ShapeDtypeStruct((rows, samples, wid...]
    all_to_all x1 -> x0, blocking collectives: 32.3 us -> none  [body(): lax.all_to_all(result, 'emb', split_axis=0, concat_axis=1, tiled=True)]
    all_gather x2 -> x0, blocking collectives: 22.3 us -> none  [gathered_by_axis(): nearer = lax.all_gather(shard, axes[-1], axis=dim, tiled=True)]
    all_to_all x1 -> x0, starting transfers between devices: 9.97 us -> none  [body(): lax.all_to_all(embeddings, 'emb', split_axis=1, concat_axis=0, tiled=True)]
    all_gather x1 -> x0, waiting for transfers between devices: 6.8 us -> none  [in_one_piece(): lax.all_gather(both, axis, axis=dim, tiled=True)]
    all_to_all x1 -> x0, waiting for transfers between devices: 6.56 us -> none  [body(): lax.all_to_all(embeddings, 'emb', split_axis=1, concat_axis=0, tiled=True)]
    dot_general x3 -> x0, matrix products: 5.97 us -> none  [the longest x1 3.15 us: body(): jnp.dot(weights_full, regrouped.reshape(emb_count, share * width), prefer...]
    all_to_all x4 -> x0, local copies, waits for them, and re-layouts: 2.72 us -> none  [the longest x2 1.65 us: body(): lax.all_to_all(result, 'emb', split_axis=0, concat_axis=1, tiled=True)]
  transfers between devices with their start and end apart: 2 -> 0, of which waited for: 2 -> 0; matrix products, arithmetic and copies ran while one was open for 8% -> 0% of each run, Pallas kernels for 0% -> 0%
where the time goes in v1:
time: 63.2 us; the launch traced here: 63.1 us
  Pallas kernels  60.8 us (96%)
  local copies, waits for them, and re-layouts  2.3 us (4%)
    pallas_call x1, Pallas kernels, body(): pl.pallas_call(kernel, out_shape=jax.ShapeDtypeStruct((rows, samples, wid...  60.8 us
    unnamed x1, local copies, waits for them, and re-layouts  2.3 us

profile of v1, /device:TPU:1, one launch (start us, length us, event | category | flops | bytes accessed | tf_op | source)
XLA Modules:
  0.0 63.1 jit_solution(9108217286198602679)
XLA Ops:
  0.0 60.8 %wukong.1 = bf16[32,64,256]{2,1,0:T(8,128)(2,1)} custom-call(bf16[32,64,256]{2,1,0:T(8,128)(2,1)} %emb_ref.1, bf16[32,512]{1,0:T(8,128)(2,1)} %bitcast.1, bf16[32,512]{1,0:T(8,128)(2,1)} %w_ref.1, bf16[32,256]{1,0:T(8,128)(2,1)} %wf_ref.1, f32[32,256]{1,0:T(8,128)} %g_ref.1, f32[32,256]{1,0:T(8,128)} %b_ref.1), custom_call_target="tpu_custom_call" | custom-call | tf_op jit(solution)/shard_map/wukong/pallas_call | solution.py:171
  60.8 2.3 %copy.8 = bf16[32,64,256]{2,1,0:T(8,128)(2,1)} copy(bf16[32,64,256]{2,1,0:T(8,128)(2,1)} %wukong.1) | data formatting | bytes 2097152

commit v2 on v1

--- a/solution.py
+++ b/solution.py
@@ -23,7 +23,8 @@
     rows, samples, width = ebuf.shape
     chunks, group = sendbuf.shape[0], sendbuf.shape[1]
     emb_count = xbuf.shape[1]
-    n_dp = w_send.shape[0] + 1
+    y, x = dp % 4, dp // 4
+    ring = (x * 4 + (y + 1) % 4, x * 4 + (y + 3) % 4, (x + 1) % 4 * 4 + y, (x + 3) % 4 * 4 + y)
 
     def peer(d, cc):
         return lax.rem(z + d, 8) * 2 + lax.rem(c + cc, 2)
@@ -31,8 +32,8 @@
     barrier = pltpu.get_barrier_semaphore()
     for d, cc in PEERS:
         pl.semaphore_signal(barrier, inc=1, device_id={"emb": peer(d, cc)}, device_id_type=MESH)
-    for k in range(1, n_dp):
-        pl.semaphore_signal(barrier, inc=1, device_id={"dp": lax.rem(dp + k, n_dp)}, device_id_type=MESH)
+    for k in range(4):
+        pl.semaphore_signal(barrier, inc=1, device_id={"dp": ring[k]}, device_id_type=MESH)
 
     def load(s):
         part = pl.ds(s * group, group)
@@ -73,18 +74,31 @@
                 device_id={"emb": j}, device_id_type=MESH,
             ).start()
 
-    def w_copy(k):
+    def w_copy(i, to, start, size):
+        part = pl.ds(pl.multiple_of(start, 16), size)
         return pltpu.make_async_remote_copy(
-            src_ref=wfull.at[my_w], dst_ref=wfull.at[my_w], send_sem=w_send.at[k - 1], recv_sem=w_recv,
-            device_id={"dp": lax.rem(dp + k, n_dp)}, device_id_type=MESH,
+            src_ref=wfull.at[part], dst_ref=wfull.at[part], send_sem=w_send.at[i], recv_sem=w_recv.at[i],
+            device_id={"dp": ring[to]}, device_id_type=MESH,
         )
+
+    column = x * 4 * rows
+    w_copies = (
+        w_copy(0, 0, column + y * rows, rows),
+        w_copy(1, 1, column + y * rows, rows),
+        w_copy(2, 0, column + (y + 3) % 4 * rows, rows // 2),
+        w_copy(3, 1, column + (y + 1) % 4 * rows + rows // 2, rows // 2),
+        w_copy(4, 2, column, 4 * rows),
+        w_copy(5, 3, column, 4 * rows),
+        w_copy(6, 2, (x + 3) % 4 * 4 * rows, 2 * rows),
+        w_copy(7, 3, (x + 1) % 4 * 4 * rows + 2 * rows, 2 * rows),
+    )
 
     prepare(0)
     own_w.wait()
-    pl.semaphore_wait(barrier, len(PEERS) + n_dp - 1)
+    pl.semaphore_wait(barrier, len(PEERS) + 4)
     send_in(0)
-    for k in range(1, n_dp):
-        w_copy(k).start()
+    w_copies[0].start()
+    w_copies[1].start()
 
     def feed(s, carry):
         prepare(s)
@@ -93,10 +107,15 @@
 
     lax.fori_loop(1, chunks, feed, 0)
 
+    for first in (0, 2, 4, 6):
+        w_copies[first].wait_recv()
+        w_copies[first + 1].wait_recv()
+        if first < 6:
+            w_copies[first + 2].start()
+            w_copies[first + 3].start()
     for copy in small:
         copy.wait()
     others = pl.ds(0, emb_count - rows)
-    pltpu.make_async_copy(wfull.at[others], wfull.at[others], w_recv).wait()
 
     block = 128
     entries = jnp.float32(emb_count * width)
@@ -157,8 +176,8 @@
         return carry
 
     lax.fori_loop(0, chunks, drain, 0)
-    for k in range(1, n_dp):
-        w_copy(k).wait_send()
+    for copy in w_copies:
+        copy.wait_send()
 
 
 def body(embeddings, machine_projection, w_lcb, w_fmb, ln_gain, ln_bias):
@@ -167,10 +186,11 @@
     group = emb_count // rows
     chunks = samples // group
     hbm = pl.BlockSpec(memory_space=pltpu.HBM)
+    operands = (embeddings, machine_projection.T, w_lcb, w_fmb, ln_gain, ln_bias)
     bf16, f32 = jnp.bfloat16, jnp.float32
     return pl.pallas_call(
         kernel,
-        out_shape=jax.ShapeDtypeStruct((rows, samples, width), bf16),
+        out_shape=pltpu.VMEM((rows, samples, width), bf16),
         in_specs=[hbm] * 6,
         out_specs=pl.BlockSpec(memory_space=pltpu.VMEM),
         scratch_shapes=[
@@ -191,14 +211,14 @@
             pltpu.SemaphoreType.DMA((chunks,)),
             pltpu.SemaphoreType.DMA((chunks,)),
             pltpu.SemaphoreType.DMA((chunks,)),
-            pltpu.SemaphoreType.DMA((emb_count // w_lcb.shape[0] - 1,)),
-            pltpu.SemaphoreType.DMA,
+            pltpu.SemaphoreType.DMA((8,)),
+            pltpu.SemaphoreType.DMA((8,)),
         ],
         compiler_params=pltpu.CompilerParams(
-            collective_id=0, has_side_effects=True, vmem_limit_bytes=67043328
+            collective_id=0, has_side_effects=True, vmem_limit_bytes=48 << 20
         ),
         name="wukong",
-    )(embeddings, machine_projection.T, w_lcb, w_fmb, ln_gain, ln_bias)
+    )(*(pltpu.with_memory_space_constraint(a, pltpu.HBM) for a in operands))
 
 
 def solution(mesh):

time: 63.2 us -> 56.6 us (0.90)
  Pallas kernels: 60.8 us -> 55.6 us
  local copies, waits for them, and re-layouts: 2.3 us -> 0.97 us
    pallas_call x1, Pallas kernels: 60.8 us -> 55.6 us  [body(): pl.pallas_call(kernel, out_shape=pltpu.VMEM((rows, samples, width), bf16)...]
    unnamed x1, local copies, waits for them, and re-layouts: 2.3 us -> 0.97 us
where the time goes in v2:
time: 56.6 us; the launch traced here: 56.5 us
  Pallas kernels  55.6 us (98%)
  local copies, waits for them, and re-layouts  0.97 us (2%)
    pallas_call x1, Pallas kernels, body(): pl.pallas_call(kernel, out_shape=pltpu.VMEM((rows, samples, width), bf16)...  55.6 us

profile of v2, /device:TPU:1, one launch (start us, length us, event | category | flops | bytes accessed | tf_op | source)
XLA Modules:
  0.0 56.5 jit_solution(2179647806700496647)
XLA Ops:
  0.0 55.6 %wukong.1 = bf16[32,64,256]{2,1,0:T(8,128)(2,1)S(1)} custom-call(bf16[32,64,256]{2,1,0:T(8,128)(2,1)} %emb_ref.1, bf16[32,512]{1,0:T(8,128)(2,1)} %bitcast.1, bf16[32,512]{1,0:T(8,128)(2,1)} %w_ref.1, bf16[32,256]{1,0:T(8,128)(2,1)} %wf_ref.1, f32[32,256]{1,0:T(8,128)} %g_ref.1, f32[32,256]{1,0:T(8,128)} %b_ref.1), custom_call_target="tpu_custom_call" | custom-call | tf_op jit(solution)/shard_map/wukong/pallas_call | solution.py:191
  55.6 1.0 %copy.8 = bf16[32,64,256]{2,1,0:T(8,128)(2,1)} copy(bf16[32,64,256]{2,1,0:T(8,128)(2,1)S(1)} %wukong.1) | data formatting | bytes 2097152

commit v3 on v2

--- a/solution.py
+++ b/solution.py
@@ -15,7 +15,7 @@
 def kernel(
     emb_ref, mp_ref, w_ref, wf_ref, g_ref, b_ref, out_ref,
     ebuf, stage, sendbuf, xbuf, wfull, rbuf, ybuf, mixed, wf_v, g_v, b_v,
-    load_sem, small_sem, in_send, in_recv, out_send, out_recv, w_send, w_recv,
+    load_sem, small_sem, in_send, in_recv, out_send, out_recv, w_send, w_recv, ready, dp_ready, told,
 ):
     e = lax.axis_index("emb")
     dp = lax.axis_index("dp")
@@ -29,11 +29,27 @@
     def peer(d, cc):
         return lax.rem(z + d, 8) * 2 + lax.rem(c + cc, 2)
 
+    def first(d, cc):
+        return c == jnp.minimum(z, 1) if d == 0 else peer(d, cc) // 2 < z
+
+    def signal(semaphore, device):
+        pl.semaphore_signal(semaphore, inc=1, device_id=device, device_id_type=MESH)
+
+    half = 4
+    late = z >= half
+
+    def apart(d, cc):
+        return jnp.logical_and(late, peer(d, cc) >= 2 * half) if d in (2, 3, 5, 6) else False
+
     barrier = pltpu.get_barrier_semaphore()
+    heard = 2 * jnp.where(late, half + jnp.minimum(z - half, 1), z) + (c == jnp.minimum(z, 1)).astype(jnp.int32)
     for d, cc in PEERS:
-        pl.semaphore_signal(barrier, inc=1, device_id={"emb": peer(d, cc)}, device_id_type=MESH)
+        pl.when(jnp.logical_not(jnp.logical_or(first(d, cc), apart(d, cc))))(functools.partial(signal, barrier, {"emb": peer(d, cc)}))
+    answers = 0
     for k in range(4):
-        pl.semaphore_signal(barrier, inc=1, device_id={"dp": ring[k]}, device_id_type=MESH)
+        pl.when(ring[k] > dp)(functools.partial(signal, barrier, {"dp": ring[k]}))
+        heard = heard + (ring[k] < dp).astype(jnp.int32)
+        answers = answers + (ring[k] > dp).astype(jnp.int32)
 
     def load(s):
         part = pl.ds(s * group, group)
@@ -41,7 +57,8 @@
 
     my_w = pl.ds(pl.multiple_of(dp * rows, rows), rows)
     load(0).start()
-    own_w = pltpu.make_async_copy(w_ref, wfull.at[my_w], small_sem.at[0])
+    my_half = pl.ds(pl.multiple_of(c * (emb_count // 2), 128), emb_count // 2)
+    own_w = pltpu.make_async_copy(w_ref.at[:, my_half], wfull.at[my_w, my_half], small_sem.at[0])
     own_w.start()
     for s in range(1, chunks):
         load(s).start()
@@ -51,6 +68,12 @@
     ]
     for copy in small:
         copy.start()
+
+    pl.when(heard > 0)(lambda: pl.semaphore_wait(barrier, heard))
+    for d, cc in PEERS:
+        pl.when(jnp.logical_and(first(d, cc), jnp.logical_not(apart(d, cc))))(functools.partial(signal, ready.at[e], {"emb": peer(d, cc)}))
+    for k in range(4):
+        pl.when(ring[k] < dp)(functools.partial(signal, dp_ready, {"dp": ring[k]}))
 
     my_rows = pl.ds(pl.multiple_of(e * rows, rows), rows)
 
@@ -65,19 +88,27 @@
                 sendbuf[s, b, :, pl.ds(h * 128, 128)] = stage[h, pl.ds(b, rows, stride=PITCH), :].astype(jnp.bfloat16)
         xbuf[s, my_rows, :] = sendbuf[s, e]
 
-    def send_in(s):
-        for i, (d, cc) in enumerate(PEERS):
-            j = peer(d, cc)
-            pltpu.make_async_remote_copy(
-                src_ref=sendbuf.at[s, j], dst_ref=xbuf.at[s, my_rows],
-                send_sem=in_send.at[s], recv_sem=in_recv.at[s],
-                device_id={"emb": j}, device_id_type=MESH,
-            ).start()
+    def send_one(s, j):
+        pltpu.make_async_remote_copy(
+            src_ref=sendbuf.at[s, j], dst_ref=xbuf.at[s, my_rows],
+            send_sem=in_send.at[s], recv_sem=in_recv.at[s],
+            device_id={"emb": j}, device_id_type=MESH,
+        ).start()
+
+    def send_to(s, to_late, to_early):
+        for d, cc in PEERS:
+            if to_late and to_early:
+                send_one(s, peer(d, cc))
+            else:
+                pl.when((peer(d, cc) >= 2 * half) == to_late)(functools.partial(send_one, s, peer(d, cc)))
+
+    def await_peer(d, cc):
+        pl.when(jnp.logical_not(first(d, cc)))(lambda: pl.semaphore_wait(ready.at[peer(d, cc)], 1))
 
     def w_copy(i, to, start, size):
         part = pl.ds(pl.multiple_of(start, 16), size)
         return pltpu.make_async_remote_copy(
-            src_ref=wfull.at[part], dst_ref=wfull.at[part], send_sem=w_send.at[i], recv_sem=w_recv.at[i],
+            src_ref=wfull.at[part, my_half], dst_ref=wfull.at[part, my_half], send_sem=w_send.at[i], recv_sem=w_recv.at[i],
             device_id={"dp": ring[to]}, device_id_type=MESH,
         )
 
@@ -93,32 +124,118 @@
         w_copy(7, 3, (x + 1) % 4 * 4 * rows + 2 * rows, 2 * rows),
     )
 
-    prepare(0)
-    own_w.wait()
-    pl.semaphore_wait(barrier, len(PEERS) + 4)
-    send_in(0)
-    w_copies[0].start()
-    w_copies[1].start()
-
-    def feed(s, carry):
-        prepare(s)
-        send_in(s)
-        return carry
-
-    lax.fori_loop(1, chunks, feed, 0)
-
-    for first in (0, 2, 4, 6):
-        w_copies[first].wait_recv()
-        w_copies[first + 1].wait_recv()
-        if first < 6:
-            w_copies[first + 2].start()
-            w_copies[first + 3].start()
+    def start_weights():
+        own_w.wait()
+        pl.when(answers > 0)(lambda: pl.semaphore_wait(dp_ready, answers))
+        w_copies[0].start()
+        w_copies[1].start()
+
+    @pl.when(jnp.logical_not(late))
+    def _():
+        def ready_made(s, carry):
+            prepare(s)
+            return carry
+
+        lax.fori_loop(0, chunks, ready_made, 0)
+        for d, cc in PEERS:
+
+            @pl.when(peer(d, cc) < 2 * half)
+            def _(d=d, cc=cc):
+                await_peer(d, cc)
+                for s in range(4):
+                    send_one(s, peer(d, cc))
+
+        start_weights()
+        for d, cc in PEERS:
+
+            @pl.when(peer(d, cc) >= 2 * half)
+            def _(d=d, cc=cc):
+                await_peer(d, cc)
+                send_one(0, peer(d, cc))
+
+        send_to(1, True, False)
+        send_to(2, True, False)
+        send_to(3, True, False)
+
+    @pl.when(late)
+    def _():
+        for s in range(2):
+            prepare(s)
+            send_to(s, False, True)
+        for s in range(2, 4):
+            prepare(s)
+
+        def tell(d, about):
+            signal(told.at[about], {"emb": peer(d, 0)})
+
+        for d, cc in PEERS[:5]:
+
+            @pl.when(peer(d, cc) >= 2 * half)
+            def _(d=d, cc=cc):
+                await_peer(d, cc)
+                send_one(0, peer(d, cc))
+
+        @pl.when(jnp.logical_and(z > half, z < 7))
+        def _():
+            tell(1, z - 1)
+            tell(7, z + 1)
+
+        start_weights()
+        for d in (6, 2, 5, 3):
+            about = lax.rem(z + d, 8)
+
+            @pl.when(apart(d, 0))
+            def _(d=d, about=about):
+                pl.semaphore_wait(told.at[about], 1)
+                if d == 6:
+                    pl.when(z == half + 2)(lambda: tell(1, about))
+                if d == 2:
+                    pl.when(z == half + 1)(lambda: tell(7, about))
+                for cc in range(2):
+                    send_one(0, peer(d, cc))
+
+        send_to(1, True, False)
+        send_to(2, True, True)
+        send_to(3, True, True)
+
+    for i in (0, 2, 4, 6):
+        w_copies[i].wait_recv()
+        w_copies[i + 1].wait_recv()
+        if i < 6:
+            w_copies[i + 2].start()
+            w_copies[i + 3].start()
+    whole = pl.ds(0, emb_count)
+    swap = pltpu.make_async_remote_copy(
+        src_ref=wfull.at[whole, my_half], dst_ref=wfull.at[whole, my_half], send_sem=w_send.at[8], recv_sem=w_recv.at[8],
+        device_id={"emb": peer(0, 1)}, device_id_type=MESH,
+    )
+    swap.start()
     for copy in small:
         copy.wait()
+    swap.wait_recv()
     others = pl.ds(0, emb_count - rows)
 
     block = 128
     entries = jnp.float32(emb_count * width)
+
+    def out_one(s, j):
+        pltpu.make_async_remote_copy(
+            src_ref=rbuf.at[s, pl.ds(pl.multiple_of(j * rows, rows), rows)], dst_ref=ybuf.at[s, e],
+            send_sem=out_send.at[s], recv_sem=out_recv.at[s],
+            device_id={"emb": j}, device_id_type=MESH,
+        ).start()
+
+    def send_out(s):
+        def relative():
+            for d, cc in PEERS:
+                out_one(s, peer(d, cc))
+
+        def absolute():
+            for j in range(16):
+                pl.when(j != e)(functools.partial(out_one, s, j))
+
+        pl.when(s < 2)(relative)
+        pl.when(s >= 2)(absolute)
 
     def mix(s, carry):
         pltpu.make_async_copy(xbuf.at[s, others], xbuf.at[s, others], in_recv.at[s]).wait()
@@ -143,13 +260,7 @@
             part = pl.ds(i * block, block)
             rbuf[s, part, :] = ((mixed[part, :] - average) * scale).astype(jnp.bfloat16)
         ybuf[s, e] = rbuf[s, my_rows, :]
-        for i, (d, cc) in enumerate(PEERS):
-            j = peer(d, cc)
-            pltpu.make_async_remote_copy(
-                src_ref=rbuf.at[s, pl.ds(pl.multiple_of(j * rows, rows), rows)], dst_ref=ybuf.at[s, e],
-                send_sem=out_send.at[s], recv_sem=out_recv.at[s],
-                device_id={"emb": j}, device_id_type=MESH,
-            ).start()
+        send_out(s)
         return carry
 
     lax.fori_loop(0, chunks, mix, 0)
@@ -178,6 +289,7 @@
     lax.fori_loop(0, chunks, drain, 0)
     for copy in w_copies:
         copy.wait_send()
+    swap.wait_send()
 
 
 def body(embeddings, machine_projection, w_lcb, w_fmb, ln_gain, ln_bias):
@@ -211,8 +323,11 @@
             pltpu.SemaphoreType.DMA((chunks,)),
             pltpu.SemaphoreType.DMA((chunks,)),
             pltpu.SemaphoreType.DMA((chunks,)),
-            pltpu.SemaphoreType.DMA((8,)),
-            pltpu.SemaphoreType.DMA((8,)),
+            pltpu.SemaphoreType.DMA((9,)),
+            pltpu.SemaphoreType.DMA((9,)),
+            pltpu.SemaphoreType.REGULAR((group,)),
+            pltpu.SemaphoreType.REGULAR,
+            pltpu.SemaphoreType.REGULAR((8,)),
         ],
         compiler_params=pltpu.CompilerParams(
             collective_id=0, has_side_effects=True, vmem_limit_bytes=48 << 20

time: 56.6 us -> 54.5 us (0.963)
  Pallas kernels: 55.6 us -> 53.5 us
    pallas_call x1, Pallas kernels: 55.6 us -> 53.5 us  [body(): pl.pallas_call(kernel, out_shape=pltpu.VMEM((rows, samples, width), bf16)...]
where the time goes in v3:
time: 54.5 us; the launch traced here: 54.4 us
  Pallas kernels  53.5 us (98%)
  local copies, waits for them, and re-layouts  0.97 us (2%)
    pallas_call x1, Pallas kernels, body(): pl.pallas_call(kernel, out_shape=pltpu.VMEM((rows, samples, width), bf16)...  53.5 us

profile of v3, /device:TPU:1, one launch (start us, length us, event | category | flops | bytes accessed | tf_op | source)
XLA Modules:
  0.0 54.4 jit_solution(9546543597791103526)
XLA Ops:
  0.0 53.5 %wukong.1 = bf16[32,64,256]{2,1,0:T(8,128)(2,1)S(1)} custom-call(bf16[32,64,256]{2,1,0:T(8,128)(2,1)} %emb_ref.1, bf16[32,512]{1,0:T(8,128)(2,1)} %bitcast.1, bf16[32,512]{1,0:T(8,128)(2,1)} %w_ref.1, bf16[32,256]{1,0:T(8,128)(2,1)} %wf_ref.1, f32[32,256]{1,0:T(8,128)} %g_ref.1, f32[32,256]{1,0:T(8,128)} %b_ref.1), custom_call_target="tpu_custom_call" | custom-call | tf_op jit(solution)/shard_map/wukong/pallas_call | solution.py:303
  53.5 1.0 %copy.8 = bf16[32,64,256]{2,1,0:T(8,128)(2,1)} copy(bf16[32,64,256]{2,1,0:T(8,128)(2,1)S(1)} %wukong.1) | data formatting | bytes 2097152

commit v4 on v3

--- a/solution.py
+++ b/solution.py
@@ -29,8 +29,17 @@
     def peer(d, cc):
         return lax.rem(z + d, 8) * 2 + lax.rem(c + cc, 2)
 
+    def load(s):
+        part = pl.ds(s * group, group)
+        return pltpu.make_async_copy(emb_ref.at[:, part], ebuf.at[:, part], load_sem.at[s])
+
+    load(0).start()
+
+    def place(chip):
+        return jnp.where(chip == 7, 11, 2 * chip)
+
     def first(d, cc):
-        return c == jnp.minimum(z, 1) if d == 0 else peer(d, cc) // 2 < z
+        return c == jnp.minimum(z, 1) if d == 0 else place(peer(d, cc) // 2) < place(z)
 
     def signal(semaphore, device):
         pl.semaphore_signal(semaphore, inc=1, device_id=device, device_id_type=MESH)
@@ -42,7 +51,7 @@
         return jnp.logical_and(late, peer(d, cc) >= 2 * half) if d in (2, 3, 5, 6) else False
 
     barrier = pltpu.get_barrier_semaphore()
-    heard = 2 * jnp.where(late, half + jnp.minimum(z - half, 1), z) + (c == jnp.minimum(z, 1)).astype(jnp.int32)
+    heard = 2 * jnp.where(late, half + jnp.where(z == half + 1, 1, jnp.where(z == half + 2, 2, 0)), z) + (c == jnp.minimum(z, 1)).astype(jnp.int32)
     for d, cc in PEERS:
         pl.when(jnp.logical_not(jnp.logical_or(first(d, cc), apart(d, cc))))(functools.partial(signal, barrier, {"emb": peer(d, cc)}))
     answers = 0
@@ -51,12 +60,7 @@
         heard = heard + (ring[k] < dp).astype(jnp.int32)
         answers = answers + (ring[k] > dp).astype(jnp.int32)
 
-    def load(s):
-        part = pl.ds(s * group, group)
-        return pltpu.make_async_copy(emb_ref.at[:, part], ebuf.at[:, part], load_sem.at[s])
-
     my_w = pl.ds(pl.multiple_of(dp * rows, rows), rows)
-    load(0).start()
     my_half = pl.ds(pl.multiple_of(c * (emb_count // 2), 128), emb_count // 2)
     own_w = pltpu.make_async_copy(w_ref.at[:, my_half], wfull.at[my_w, my_half], small_sem.at[0])
     own_w.start()
@@ -91,7 +95,7 @@
     def send_one(s, j):
         pltpu.make_async_remote_copy(
             src_ref=sendbuf.at[s, j], dst_ref=xbuf.at[s, my_rows],
-            send_sem=in_send.at[s], recv_sem=in_recv.at[s],
+            send_sem=in_send, recv_sem=in_recv.at[s],
             device_id={"emb": j}, device_id_type=MESH,
         ).start()
 
@@ -108,7 +112,7 @@
     def w_copy(i, to, start, size):
         part = pl.ds(pl.multiple_of(start, 16), size)
         return pltpu.make_async_remote_copy(
-            src_ref=wfull.at[part, my_half], dst_ref=wfull.at[part, my_half], send_sem=w_send.at[i], recv_sem=w_recv.at[i],
+            src_ref=wfull.at[part, my_half], dst_ref=wfull.at[part, my_half], send_sem=w_send, recv_sem=w_recv.at[i],
             device_id={"dp": ring[to]}, device_id_type=MESH,
         )
 
@@ -166,7 +170,7 @@
             prepare(s)
 
         def tell(d, about):
-            signal(told.at[about], {"emb": peer(d, 0)})
+            signal(told.at[about - half], {"emb": peer(d, 0)})
 
         for d, cc in PEERS[:5]:
 
@@ -186,7 +190,7 @@
 
             @pl.when(apart(d, 0))
             def _(d=d, about=about):
-                pl.semaphore_wait(told.at[about], 1)
+                pl.semaphore_wait(told.at[about - half], 1)
                 if d == 6:
                     pl.when(z == half + 2)(lambda: tell(1, about))
                 if d == 2:
@@ -206,7 +210,7 @@
             w_copies[i + 3].start()
     whole = pl.ds(0, emb_count)
     swap = pltpu.make_async_remote_copy(
-        src_ref=wfull.at[whole, my_half], dst_ref=wfull.at[whole, my_half], send_sem=w_send.at[8], recv_sem=w_recv.at[8],
+        src_ref=wfull.at[whole, my_half], dst_ref=wfull.at[whole, my_half], send_sem=w_send, recv_sem=w_recv.at[8],
         device_id={"emb": peer(0, 1)}, device_id_type=MESH,
     )
     swap.start()
@@ -221,7 +225,7 @@
     def out_one(s, j):
         pltpu.make_async_remote_copy(
             src_ref=rbuf.at[s, pl.ds(pl.multiple_of(j * rows, rows), rows)], dst_ref=ybuf.at[s, e],
-            send_sem=out_send.at[s], recv_sem=out_recv.at[s],
+            send_sem=out_send, recv_sem=out_recv.at[s],
             device_id={"emb": j}, device_id_type=MESH,
         ).start()
 
@@ -233,6 +237,18 @@
         def absolute():
             for j in range(16):
                 pl.when(j != e)(functools.partial(out_one, s, j))
+
+        def across(nearest):
+            if nearest:
+                for d, cc in PEERS:
+                    pl.when((peer(d, cc) >= 2 * half) != late)(functools.partial(out_one, s, peer(d, cc)))
+            else:
+                for j in range(2 * half):
+                    pl.when(late)(functools.partial(out_one, s, j))
+                for d, cc in PEERS:
+                    pl.when(jnp.logical_and(peer(d, cc) >= 2 * half, jnp.logical_not(late)))(functools.partial(out_one, s, peer(d, cc)))
+            for j in range(4 * half):
+                pl.when(jnp.logical_and(j != e, (j >= 2 * half) == late))(functools.partial(out_one, s, j))
 
         pl.when(s < 2)(relative)
         pl.when(s >= 2)(absolute)
@@ -281,15 +297,12 @@
 
     lax.fori_loop(0, chunks, finish, 0)
 
-    def drain(s, carry):
-        pltpu.make_async_copy(sendbuf.at[s, fifteen], sendbuf.at[s, fifteen], in_send.at[s]).wait()
-        pltpu.make_async_copy(ybuf.at[s, fifteen], ybuf.at[s, fifteen], out_send.at[s]).wait()
-        return carry
-
-    lax.fori_loop(0, chunks, drain, 0)
-    for copy in w_copies:
-        copy.wait_send()
-    swap.wait_send()
+    sent = pltpu.make_async_copy(sendbuf.at[:, fifteen], sendbuf.at[:, fifteen], in_send)
+    sent.wait()
+    sent = pltpu.make_async_copy(ybuf.at[:, fifteen], ybuf.at[:, fifteen], out_send)
+    sent.wait()
+    passed = pl.ds(0, emb_count - rows // 2)
+    pltpu.make_async_copy(wfull.at[passed], wfull.at[passed], w_send).wait()
 
 
 def body(embeddings, machine_projection, w_lcb, w_fmb, ln_gain, ln_bias):
@@ -319,15 +332,15 @@
             pltpu.VMEM(ln_bias.shape, f32),
             pltpu.SemaphoreType.DMA((chunks,)),
             pltpu.SemaphoreType.DMA((5,)),
+            pltpu.SemaphoreType.DMA,
             pltpu.SemaphoreType.DMA((chunks,)),
+            pltpu.SemaphoreType.DMA,
             pltpu.SemaphoreType.DMA((chunks,)),
-            pltpu.SemaphoreType.DMA((chunks,)),
-            pltpu.SemaphoreType.DMA((chunks,)),
-            pltpu.SemaphoreType.DMA((9,)),
+            pltpu.SemaphoreType.DMA,
             pltpu.SemaphoreType.DMA((9,)),
             pltpu.SemaphoreType.REGULAR((group,)),
             pltpu.SemaphoreType.REGULAR,
-            pltpu.SemaphoreType.REGULAR((8,)),
+            pltpu.SemaphoreType.REGULAR((4,)),
         ],
         compiler_params=pltpu.CompilerParams(
             collective_id=0, has_side_effects=True, vmem_limit_bytes=48 << 20

time: 54.5 us -> 54.4 us (level)
  no operation moved by 1% of the time
where the time goes in v4:
time: 54.4 us; the launch traced here: 54.3 us
  Pallas kernels  53.3 us (98%)
  local copies, waits for them, and re-layouts  0.97 us (2%)
    pallas_call x1, Pallas kernels, body(): pl.pallas_call(kernel, out_shape=pltpu.VMEM((rows, samples, width), bf16)...  53.3 us

profile of v4, /device:TPU:1, one launch (start us, length us, event | category | flops | bytes accessed | tf_op | source)
XLA Modules:
  0.0 54.3 jit_solution(3567482450187777073)
XLA Ops:
  0.0 53.3 %wukong.1 = bf16[32,64,256]{2,1,0:T(8,128)(2,1)S(1)} custom-call(bf16[32,64,256]{2,1,0:T(8,128)(2,1)} %emb_ref.1, bf16[32,512]{1,0:T(8,128)(2,1)} %bitcast.1, bf16[32,512]{1,0:T(8,128)(2,1)} %w_ref.1, bf16[32,256]{1,0:T(8,128)(2,1)} %wf_ref.1, f32[32,256]{1,0:T(8,128)} %g_ref.1, f32[32,256]{1,0:T(8,128)} %b_ref.1), custom_call_target="tpu_custom_call" | custom-call | tf_op jit(solution)/shard_map/wukong/pallas_call | solution.py:316
  53.3 1.0 %copy.8 = bf16[32,64,256]{2,1,0:T(8,128)(2,1)} copy(bf16[32,64,256]{2,1,0:T(8,128)(2,1)S(1)} %wukong.1) | data formatting | bytes 2097152

commit v5 on v4

--- a/solution.py
+++ b/solution.py
@@ -21,6 +21,7 @@
     dp = lax.axis_index("dp")
     z, c = e // 2, e % 2
     rows, samples, width = ebuf.shape
+    rank = mp_ref.shape[0]
     chunks, group = sendbuf.shape[0], sendbuf.shape[1]
     emb_count = xbuf.shape[1]
     y, x = dp % 4, dp // 4
@@ -67,7 +68,7 @@
     for s in range(1, chunks):
         load(s).start()
     small = [
-        pltpu.make_async_copy(a, v, small_sem.at[1 + i])
+        pltpu.make_async_copy(a, v, small_sem.at[1])
         for i, (a, v) in enumerate(((mp_ref, wfull.at[pl.ds(emb_count, mp_ref.shape[0])]), (wf_ref, wf_v), (g_ref, g_v), (b_ref, b_v)))
     ]
     for copy in small:
@@ -112,7 +113,7 @@
     def w_copy(i, to, start, size):
         part = pl.ds(pl.multiple_of(start, 16), size)
         return pltpu.make_async_remote_copy(
-            src_ref=wfull.at[part, my_half], dst_ref=wfull.at[part, my_half], send_sem=w_send, recv_sem=w_recv.at[i],
+            src_ref=wfull.at[part, my_half], dst_ref=wfull.at[part, my_half], send_sem=w_send, recv_sem=w_recv.at[i // 2],
             device_id={"dp": ring[to]}, device_id_type=MESH,
         )
 
@@ -203,19 +204,19 @@
         send_to(3, True, True)
 
     for i in (0, 2, 4, 6):
-        w_copies[i].wait_recv()
-        w_copies[i + 1].wait_recv()
+        both = pl.ds(0, rows * (2, 1, 8, 4)[i // 2] // 2)
+        pltpu.make_async_copy(wfull.at[both], wfull.at[both], w_recv.at[i // 2]).wait()
         if i < 6:
             w_copies[i + 2].start()
             w_copies[i + 3].start()
     whole = pl.ds(0, emb_count)
     swap = pltpu.make_async_remote_copy(
-        src_ref=wfull.at[whole, my_half], dst_ref=wfull.at[whole, my_half], send_sem=w_send, recv_sem=w_recv.at[8],
+        src_ref=wfull.at[whole, my_half], dst_ref=wfull.at[whole, my_half], send_sem=w_send, recv_sem=w_recv.at[4],
         device_id={"emb": peer(0, 1)}, device_id_type=MESH,
     )
     swap.start()
-    for copy in small:
-        copy.wait()
+    loaded = pl.ds(0, 7 * rank // 2)
+    pltpu.make_async_copy(wfull.at[loaded], wfull.at[loaded], small_sem.at[1]).wait()
     swap.wait_recv()
     others = pl.ds(0, emb_count - rows)
 
@@ -234,24 +235,7 @@
             for d, cc in PEERS:
                 out_one(s, peer(d, cc))
 
-        def absolute():
-            for j in range(16):
-                pl.when(j != e)(functools.partial(out_one, s, j))
-
-        def across(nearest):
-            if nearest:
-                for d, cc in PEERS:
-                    pl.when((peer(d, cc) >= 2 * half) != late)(functools.partial(out_one, s, peer(d, cc)))
-            else:
-                for j in range(2 * half):
-                    pl.when(late)(functools.partial(out_one, s, j))
-                for d, cc in PEERS:
-                    pl.when(jnp.logical_and(peer(d, cc) >= 2 * half, jnp.logical_not(late)))(functools.partial(out_one, s, peer(d, cc)))
-            for j in range(4 * half):
-                pl.when(jnp.logical_and(j != e, (j >= 2 * half) == late))(functools.partial(out_one, s, j))
-
         pl.when(s < 2)(relative)
-        pl.when(s >= 2)(absolute)
 
     def mix(s, carry):
         pltpu.make_async_copy(xbuf.at[s, others], xbuf.at[s, others], in_recv.at[s]).wait()
@@ -280,11 +264,48 @@
         return carry
 
     lax.fori_loop(0, chunks, mix, 0)
+    held = jnp.logical_and(z > 0, jnp.logical_not(late))
+    second = jnp.logical_and(z == 0, c == 1)
+
+    @pl.when(z > 0)
+    def _():
+        for chip, parts in ((2, (2,)), (1, (2,)), (0, (2, 3)), (1, (3,)), (2, (3,)), (3, (2, 3)), (4, (2, 3)), (5, (2, 3)), (6, (2, 3)), (7, (2, 3))):
+            for j in (2 * chip, 2 * chip + 1):
+
+                @pl.when(jnp.logical_and(j != e, jnp.logical_not(held)) if j in (12, 13, 14, 15) else j != e)
+                def _(j=j, parts=parts):
+                    for s in parts:
+                        out_one(s, j)
+
+    @pl.when(z == 0)
+    def _():
+        for chip in (5, 6, 7, 4, 1, 2, 3, 0):
+            for j in (2 * chip, 2 * chip + 1):
+
+                @pl.when(jnp.logical_and(j != e, jnp.logical_not(second)) if chip in (7,) else j != e)
+                def _(j=j):
+                    for s in range(2, 4):
+                        out_one(s, j)
+
 
     fifteen = pl.ds(0, group - 1)
 
     def finish(s, carry):
         pltpu.make_async_copy(ybuf.at[s, fifteen], ybuf.at[s, fifteen], out_recv.at[s]).wait()
+
+        @pl.when(jnp.logical_and(held, s == 1))
+        def _():
+            for j in (12, 13, 14, 15):
+                for t in range(2, 4):
+                    out_one(t, j)
+
+        @pl.when(jnp.logical_and(second, s == 1))
+        def _():
+            for chip in (7,):
+                for j in (2 * chip, 2 * chip + 1):
+                    for t in range(2, 4):
+                        out_one(t, j)
+
         part = pl.ds(pl.multiple_of(s * group, group), group)
         for b in range(group):
             y = ybuf[s, b].astype(jnp.float32) * g_v[...] + b_v[...]
@@ -331,13 +352,13 @@
             pltpu.VMEM(ln_gain.shape, f32),
             pltpu.VMEM(ln_bias.shape, f32),
             pltpu.SemaphoreType.DMA((chunks,)),
-            pltpu.SemaphoreType.DMA((5,)),
+            pltpu.SemaphoreType.DMA((2,)),
             pltpu.SemaphoreType.DMA,
             pltpu.SemaphoreType.DMA((chunks,)),
             pltpu.SemaphoreType.DMA,
             pltpu.SemaphoreType.DMA((chunks,)),
             pltpu.SemaphoreType.DMA,
-            pltpu.SemaphoreType.DMA((9,)),
+            pltpu.SemaphoreType.DMA((5,)),
             pltpu.SemaphoreType.REGULAR((group,)),
             pltpu.SemaphoreType.REGULAR,
             pltpu.SemaphoreType.REGULAR((4,)),

time: 54.4 us -> 54.1 us (level)
  Pallas kernels: 53.3 us -> 52.7 us
    pallas_call x1, Pallas kernels: 53.3 us -> 52.7 us  [body(): pl.pallas_call(kernel, out_shape=pltpu.VMEM((rows, samples, width), bf16)...]
where the time goes in v5:
time: 54.1 us; the launch traced here: 53.7 us
  Pallas kernels  52.7 us (97%)
  local copies, waits for them, and re-layouts  0.97 us (2%)
    pallas_call x1, Pallas kernels, body(): pl.pallas_call(kernel, out_shape=pltpu.VMEM((rows, samples, width), bf16)...  52.7 us

profile of v5, /device:TPU:1, one launch (start us, length us, event | category | flops | bytes accessed | tf_op | source)
XLA Modules:
  0.0 53.7 jit_solution(17228563871025291803)
XLA Ops:
  0.0 52.7 %wukong.1 = bf16[32,64,256]{2,1,0:T(8,128)(2,1)S(1)} custom-call(bf16[32,64,256]{2,1,0:T(8,128)(2,1)} %emb_ref.1, bf16[32,512]{1,0:T(8,128)(2,1)} %bitcast.1, bf16[32,512]{1,0:T(8,128)(2,1)} %w_ref.1, bf16[32,256]{1,0:T(8,128)(2,1)} %wf_ref.1, f32[32,256]{1,0:T(8,128)} %g_ref.1, f32[32,256]{1,0:T(8,128)} %b_ref.1), custom_call_target="tpu_custom_call" | custom-call | tf_op jit(solution)/shard_map/wukong/pallas_call | solution.py:337
  52.7 1.0 %copy.8 = bf16[32,64,256]{2,1,0:T(8,128)(2,1)} copy(bf16[32,64,256]{2,1,0:T(8,128)(2,1)S(1)} %wukong.1) | data formatting | bytes 2097152

commit v6 on v5

--- a/solution.py
+++ b/solution.py
@@ -82,15 +82,21 @@
 
     my_rows = pl.ds(pl.multiple_of(e * rows, rows), rows)
 
-    def prepare(s):
+    def arrange(s, blocks):
+        for b in blocks:
+            for h in range(2):
+                sendbuf[s, b, :, pl.ds(h * 128, 128)] = stage[h, pl.ds(b, rows, stride=PITCH), :].astype(jnp.bfloat16)
+
+    def stage_in(s):
         load(s).wait()
         for n in range(rows):
             block = ebuf[n, pl.ds(pl.multiple_of(s * group, group), group), :].astype(jnp.float32)
             for h in range(2):
                 stage[h, pl.ds(n * PITCH, group), :] = block[:, h * 128 : (h + 1) * 128]
-        for b in range(group):
-            for h in range(2):
-                sendbuf[s, b, :, pl.ds(h * 128, 128)] = stage[h, pl.ds(b, rows, stride=PITCH), :].astype(jnp.bfloat16)
+
+    def prepare(s):
+        stage_in(s)
+        arrange(s, range(group))
         xbuf[s, my_rows, :] = sendbuf[s, e]
 
     def send_one(s, j):
@@ -164,9 +170,13 @@
 
     @pl.when(late)
     def _():
-        for s in range(2):
-            prepare(s)
-            send_to(s, False, True)
+        stage_in(0)
+        arrange(0, range(2 * half))
+        send_to(0, False, True)
+        arrange(0, range(2 * half, group))
+        xbuf[0, my_rows, :] = sendbuf[0, e]
+        prepare(1)
+        send_to(1, False, True)
         for s in range(2, 4):
             prepare(s)
 

time: 54.1 us -> 54.1 us (level)
  no operation moved by 1% of the time
where the time goes in v6:
time: 54.1 us; the launch traced here: 53.7 us
  Pallas kernels  52.7 us (97%)
  local copies, waits for them, and re-layouts  0.97 us (2%)
    pallas_call x1, Pallas kernels, body(): pl.pallas_call(kernel, out_shape=pltpu.VMEM((rows, samples, width), bf16)...  52.7 us

profile of v6, /device:TPU:1, one launch (start us, length us, event | category | flops | bytes accessed | tf_op | source)
XLA Modules:
  0.0 53.7 jit_solution(10649722259802743600)
XLA Ops:
  0.0 52.7 %wukong.1 = bf16[32,64,256]{2,1,0:T(8,128)(2,1)S(1)} custom-call(bf16[32,64,256]{2,1,0:T(8,128)(2,1)} %emb_ref.1, bf16[32,512]{1,0:T(8,128)(2,1)} %bitcast.1, bf16[32,512]{1,0:T(8,128)(2,1)} %w_ref.1, bf16[32,256]{1,0:T(8,128)(2,1)} %wf_ref.1, f32[32,256]{1,0:T(8,128)} %g_ref.1, f32[32,256]{1,0:T(8,128)} %b_ref.1), custom_call_target="tpu_custom_call" | custom-call | tf_op jit(solution)/shard_map/wukong/pallas_call | solution.py:347
  52.7 1.0 %copy.8 = bf16[32,64,256]{2,1,0:T(8,128)(2,1)} copy(bf16[32,64,256]{2,1,0:T(8,128)(2,1)S(1)} %wukong.1) | data formatting | bytes 2097152
